TPU v7x, 256 devices: a whole 4x4x8 slice. The times are simulated.
256 devices in a mesh: row: 4 (over x), col: 2 (over core), dp: 32 (over z, y).
Axes of the slice: x: 4, y: 4, z: 8, core: 2. Of those that a mesh axis runs over, the one named last changes fastest.
Arguments:
- out_grad: bfloat16 [32, 128, 4096], P('dp', 'col', 'row'), may hold values from -6 to 6
- saved_hidden: bfloat16 [32, 128, 14336], P('dp', 'row', 'col'), may hold values from -6 to 6
- down_weight: bfloat16 [14336, 4096], P(('col', 'dp'), 'row'), may hold values from -0.046875 to 0.046875
Outputs:
- hidden_grad: bfloat16 [32, 128, 14336], P('dp', 'row', 'col')
- weight_grad: bfloat16 [14336, 4096], P(('col', 'dp'), 'row')
All inputs are finite; a program needn't handle non-finite values.
Results may differ from a plain program's by a relative error of at most 0.009.
Values may be sent and summed in bfloat16 or wider, within the bound.
No kernel may reach another device: no remote copies, remote signals or barrier semaphores. Data moves between devices by JAX's collectives and lax.ppermute only.
A program may use at most 64 MiB of HBM per device.

v0:
```python
import jax
import jax.numpy as jnp
from jax import lax
from jax.sharding import Mesh
from jax.sharding import PartitionSpec as P

DP = ("dp_0", "dp_1")
COL_DP = ("col", "dp_0", "dp_1")


def sent_to_all(value, axis):
    devices = lax.axis_size(axis)
    return lax.all_to_all(
        jnp.broadcast_to(value[None], (devices, *value.shape)), axis, 0, 0, tiled=True
    )


def in_order(parts, dim):
    shape = list(parts.shape[1:])
    shape[dim] *= parts.shape[0]
    return jnp.moveaxis(parts, 0, dim).reshape(shape)


def gathered_copies(value, axis, dim):
    parts = sent_to_all(value, axis)
    return in_order(parts, dim)


def cut_along(value, dim, devices):
    shape = value.shape
    parts = value.reshape(*shape[:dim], devices, shape[dim] // devices, *shape[dim + 1 :])
    return jnp.moveaxis(parts, dim, 0)


def exchange_in_order(parts, axes, order):
    inside = parts.shape[1:]
    out = parts.reshape(*(lax.axis_size(a) for a in axes), *inside)
    for k in order:
        out = lax.all_to_all(out, axes[k], k, k, tiled=True)
    return out.reshape(-1, *inside)


def one_axis_at_a_time(value, axes, order, split_dim, concat_dim):
    parts = cut_along(value, split_dim, lax.axis_size(axes))
    return in_order(exchange_in_order(parts, axes, order), concat_dim)


def sent_and_summed(value, axis, dim):
    devices = lax.axis_size(axis)
    parts = lax.all_to_all(cut_along(value, dim, devices), axis, 0, 0, tiled=True)
    return jnp.sum(parts.astype(jnp.float32), axis=0)


def on_device(out_grad, saved_hidden, down_weight):
    grad_local = out_grad[0]
    hidden_local = saved_hidden[0]
    units = down_weight.shape[0]
    width = down_weight.shape[1]
    grad_replica = gathered_copies(grad_local, "col", 0)
    grad_all = lax.all_gather(grad_replica[:, None, :], DP, axis=1, tiled=True)
    tok_count = grad_all.shape[0]
    replica_count = grad_all.shape[1]
    local_tokens = hidden_local.shape[0]
    hidden_units = one_axis_at_a_time(hidden_local[:, None, :], DP, (0, 1), 2, 1)
    factor = jnp.float32(1.0) / jnp.sqrt(jnp.float32(tok_count * replica_count))
    flat_grad = grad_all.reshape(tok_count * replica_count, width)
    rows = flat_grad
    summed = sent_and_summed(
        lax.dot_general(
            rows, down_weight, (((1,), (1,)), ((), ())), preferred_element_type=jnp.float32
        ).astype(jnp.bfloat16),
        "row",
        0,
    )
    local_grad = summed.astype(jnp.bfloat16).reshape(local_tokens, replica_count, units)
    returned = lax.all_to_all(local_grad, DP, split_axis=1, concat_axis=2, tiled=True)
    hidden_grad = returned.reshape(1, local_tokens, -1)
    rows = grad_all
    left = gathered_copies(hidden_units, "row", 0).reshape(-1, units)
    right = rows.reshape(-1, width)
    total = lax.dot_general(
        left, right, (((0,), (0,)), ((), ())), preferred_element_type=jnp.float32
    )
    weight_grad = (total * factor).astype(jnp.bfloat16)
    return (hidden_grad, weight_grad)


def solution(mesh):
    split = Mesh(
        mesh.devices.reshape(mesh.shape["row"], mesh.shape["col"], 8, 4),
        ("row", "col", "dp_0", "dp_1"),
    )
    in_specs = (P(DP, "col", "row"), P(DP, "row", "col"), P(COL_DP, "row"))
    out_specs = (P(DP, "row", "col"), P(COL_DP, "row"))
    return jax.shard_map(
        on_device, mesh=split, in_specs=in_specs, out_specs=out_specs, check_vma=False
    )
```

profile of v0, /device:TPU:32, one launch (start us, length us, event | category | flops | bytes accessed | tf_op | source)
XLA Modules:
  0.0 220.8 jit_solution(18333720154147256579)
XLA Ops:
  7.2 0.0 copy-start
  7.2 0.0 all-gather.2.cloned.1.call-start
  7.2 1.0 broadcast_in_dim.15
  8.2 4.7 %all_to_all.34 = bf16[2,64,1024]{2,1,0:T(8,128)(2,1)} all-to-all(bf16[2,64,1024]{2,1,0:T(8,128)(2,1)S(1)} %broadcast_in_dim.15), channel_id=1, replica_groups=mesh['row'=4,'col'=2,'dp_0'=8,'dp_1'=4] {'col'}, dimensions={0} | all-to-all | bytes 524288 | tf_op jit(solution)/shard_map/all_to_all | solution.py:13
  12.9 0.0 all-gather.2.cloned.1.call-update
  12.9 1.8 reshape_broadcast_in_dim_squeeze.3
  14.7 0.3 copy.28
  15.0 0.4 copy.29
  15.4 27.7 %all_to_all.35 = bf16[8,4,32,1,224]{4,1,2,3,0:T(4,128)(2,1)S(1)} all-to-all(bf16[8,4,32,1,224]{4,1,2,3,0:T(4,128)(2,1)S(1)} %copy.29), channel_id=1, replica_groups=mesh['row'=4,'col'=2,'dp_0'=8,'dp_1'=4] {'dp_0'}, dimensions={0} | all-to-all | bytes 917504 | tf_op jit(solution)/shard_map/all_to_all | solution.py:39
  43.1 1.1 copy.30
  44.2 4.7 %all-to-all-start.4 = ((bf16[8,4,32,1,224]{4,0,2,3,1:T(8,128)(2,1)}), bf16[8,4,32,1,224]{4,0,2,3,1:T(8,128)(2,1)S(1)}, u32[]{:S(2)}, u32[]{:S(2)}) async-start(bf16[8,4,32,1,224]{4,0,2,3,1:T(8,128)(2,1)} %copy.30), calls=%async_computation.4 | async-start | bytes 1048576 | tf_op jit(solution)/shard_map/all_to_all | solution.py:39
  48.9 65.0 %all-gather.2.cloned.1.call-done = bf16[128,32,1024]{2,0,1:T(8,128)(2,1)} async-done(((bf16[128,1,1024]{2,0,1:T(8,128)(2,1)}), bf16[128,32,1024]{2,0,1:T(8,128)(2,1)}) %all-gather.2.cloned.1.call-update) | async-done | bytes 8388624 | tf_op jit(solution)/shard_map/all_gather | solution.py:60
  113.9 11.3 %copy.22 = bf16[128,32,1024]{2,1,0:T(8,128)(2,1)} copy(bf16[128,32,1024]{2,0,1:T(8,128)(2,1)} %all-gather.2.cloned.1.call-done) | data formatting | bytes 16777216 | tf_op jit(solution)/shard_map/all_gather | solution.py:60
  125.2 0.0 copy-done
  125.2 6.0 %convolution_convert_fusion = bf16[4096,224]{0,1:T(8,128)(2,1)S(1)} fusion(bf16[4096,1024]{1,0:T(8,128)(2,1)} %bitcast.21, bf16[224,1024]{1,0:T(8,128)(2,1)S(1)} %copy-done), kind=kOutput, calls=%fused_computation | convolution fusion | flops 1879965696 | bytes 10682368 | tf_op jit(solution)/shard_map/dot_general | solution.py:69
  131.2 1.5 copy.37
  132.7 0.0 all-to-all-done.4
  132.7 4.3 %all-to-all-start.1 = ((bf16[4,1024,224]{1,2,0:T(8,128)(2,1)}), bf16[4,1024,224]{1,2,0:T(8,128)(2,1)S(1)}, u32[]{:S(2)}, u32[]{:S(2)}) async-start(bf16[4,1024,224]{1,2,0:T(8,128)(2,1)} %bitcast.24), calls=%async_computation.1 | async-start | bytes 3670016 | tf_op jit(solution)/shard_map/all_to_all | solution.py:50
  137.0 0.1 copy.31
  137.1 0.3 copy.38
  137.4 22.5 %all-to-all-done.1 = bf16[4,1024,224]{1,2,0:T(8,128)(2,1)S(1)} async-done(((bf16[4,1024,224]{1,2,0:T(8,128)(2,1)}), bf16[4,1024,224]{1,2,0:T(8,128)(2,1)S(1)}, u32[]{:S(2)}, u32[]{:S(2)}) %all-to-all-start.1) | async-done | bytes 1835040 | tf_op jit(solution)/shard_map/all_to_all | solution.py:50
  159.9 0.0 copy-start.1
  159.9 1.8 broadcast_in_dim.17
  161.7 0.1 copy-done.1
  161.8 3.6 %all-to-all-start.5 = ((bf16[4,32,32,224]{3,2,1,0:T(8,128)(2,1)}), bf16[4,32,32,224]{3,2,1,0:T(8,128)(2,1)S(1)}, u32[]{:S(2)}, u32[]{:S(2)}) async-start(bf16[4,32,32,224]{3,2,1,0:T(8,128)(2,1)} %broadcast_in_dim.17), calls=%async_computation.5 | async-start | bytes 4194304 | tf_op jit(solution)/shard_map/all_to_all | solution.py:13
  165.4 1.9 reduce_sum.12
  167.3 0.2 copy.25
  167.5 1.1 copy.26
  168.6 21.7 %all-to-all-done.5 = bf16[4,32,32,224]{3,2,1,0:T(8,128)(2,1)S(1)} async-done(((bf16[4,32,32,224]{3,2,1,0:T(8,128)(2,1)}), bf16[4,32,32,224]{3,2,1,0:T(8,128)(2,1)S(1)}, u32[]{:S(2)}, u32[]{:S(2)}) %all-to-all-start.5) | async-done | bytes 1835040 | tf_op jit(solution)/shard_map/all_to_all | solution.py:13
  190.3 7.1 %all-to-all-start.2 = ((bf16[32,32,224]{2,0,1:T(8,128)(2,1)}), bf16[32,32,224]{2,0,1:T(8,128)(2,1)S(1)}, u32[]{:S(2)}, u32[]{:S(2)}) async-start(bf16[32,32,224]{2,0,1:T(8,128)(2,1)} %copy.26), calls=%async_computation.2 | async-start | bytes 1048576 | tf_op jit(solution)/shard_map/all_to_all | solution.py:76
  197.4 6.2 %fusion = bf16[224,1024]{1,0:T(8,128)(2,1)} fusion(bf16[4096,224]{1,0:T(8,128)(2,1)S(1)} %bitcast.23, bf16[4096,1024]{1,0:T(8,128)(2,1)} %bitcast.22), kind=kOutput, calls=%fused_computation.3 | convolution fusion | flops 1879506944 | bytes 10682368 | tf_op jit(solution)/shard_map/dot_general | solution.py:81
  203.7 8.3 %all-to-all-done.2 = bf16[32,32,224]{2,0,1:T(8,128)(2,1)S(1)} async-done(((bf16[32,32,224]{2,0,1:T(8,128)(2,1)}), bf16[32,32,224]{2,0,1:T(8,128)(2,1)S(1)}, u32[]{:S(2)}, u32[]{:S(2)}) %all-to-all-start.2) | async-done | bytes 458784 | tf_op jit(solution)/shard_map/all_to_all | solution.py:76
  212.0 0.3 copy.27
  212.3 1.6 reshape.31
Async XLA Ops:
  7.2 118.0 %copy-start = (bf16[224,1024]{1,0:T(8,128)(2,1)S(1)}, bf16[224,1024]{1,0:T(8,128)(2,1)}, u32[]{:S(2)}) copy-start(bf16[224,1024]{1,0:T(8,128)(2,1)} %param.5) | copy-start | bytes 1376260
  7.2 106.7 %all-gather.2.cloned.1.call-start = ((), (), s32[]{:S(2)}) async-start(), calls=%async_computation.6 | async-start | bytes 8650752 | tf_op jit(solution)/shard_map/all_gather | solution.py:60
  44.2 88.5 %all-to-all-start.4 = ((bf16[8,4,32,1,224]{4,0,2,3,1:T(8,128)(2,1)}), bf16[8,4,32,1,224]{4,0,2,3,1:T(8,128)(2,1)S(1)}, u32[]{:S(2)}, u32[]{:S(2)}) async-start(bf16[8,4,32,1,224]{4,0,2,3,1:T(8,128)(2,1)} %copy.30), calls=%async_computation.4 | async-start | bytes 1048576 | tf_op jit(solution)/shard_map/all_to_all | solution.py:39
  132.7 27.2 %all-to-all-start.1 = ((bf16[4,1024,224]{1,2,0:T(8,128)(2,1)}), bf16[4,1024,224]{1,2,0:T(8,128)(2,1)S(1)}, u32[]{:S(2)}, u32[]{:S(2)}) async-start(bf16[4,1024,224]{1,2,0:T(8,128)(2,1)} %bitcast.24), calls=%async_computation.1 | async-start | bytes 3670016 | tf_op jit(solution)/shard_map/all_to_all | solution.py:50
  159.9 1.9 copy-start.1
  161.8 28.5 %all-to-all-start.5 = ((bf16[4,32,32,224]{3,2,1,0:T(8,128)(2,1)}), bf16[4,32,32,224]{3,2,1,0:T(8,128)(2,1)S(1)}, u32[]{:S(2)}, u32[]{:S(2)}) async-start(bf16[4,32,32,224]{3,2,1,0:T(8,128)(2,1)} %broadcast_in_dim.17), calls=%async_computation.5 | async-start | bytes 4194304 | tf_op jit(solution)/shard_map/all_to_all | solution.py:13
  190.3 21.7 %all-to-all-start.2 = ((bf16[32,32,224]{2,0,1:T(8,128)(2,1)}), bf16[32,32,224]{2,0,1:T(8,128)(2,1)S(1)}, u32[]{:S(2)}, u32[]{:S(2)}) async-start(bf16[32,32,224]{2,0,1:T(8,128)(2,1)} %copy.26), calls=%async_computation.2 | async-start | bytes 1048576 | tf_op jit(solution)/shard_map/all_to_all | solution.py:76
Sparse Core Ops, SparseCore 0:
  13.0 100.8 all-gather.1
where the time goes:
time: 221 us
  waiting for transfers between devices  118 us (53%)
  blocking collectives  32.4 us (15%)
  local copies, waits for them, and re-layouts  22.8 us (10%)
  starting transfers between devices  19.8 us (9%)
  between operations  14.1 us (6%)
  matrix products  12.2 us (6%)
    all_gather x1, waiting for transfers between devices, on_device(): grad_all = lax.all_gather(grad_replica[:, None, :], DP, axis=1, tiled=True)  65 us
    all_to_all x1, blocking collectives, exchange_in_order(): out = lax.all_to_all(out, axes[k], k, k, tiled=True)  27.7 us
    all_to_all x1, waiting for transfers between devices, sent_and_summed(): lax.all_to_all(cut_along(value, dim, devices), axis, 0, 0, tiled=True)  22.5 us
    all_to_all x1, waiting for transfers between devices, sent_to_all(): lax.all_to_all(jnp.broadcast_to(value[None], (devices, *value.shape)), ax...  21.7 us
    all_gather x1, local copies, waits for them, and re-layouts, on_device(): grad_all = lax.all_gather(grad_replica[:, None, :], DP, axis=1, tiled=True)  11.3 us
    all_to_all x1, waiting for transfers between devices, on_device(): lax.all_to_all(local_grad, DP, split_axis=1, concat_axis=2, tiled=True)  8.33 us
    all_to_all x1, starting transfers between devices, on_device(): lax.all_to_all(local_grad, DP, split_axis=1, concat_axis=2, tiled=True)  7.13 us
    dot_general x1, matrix products, on_device(): lax.dot_general(left, right, (((0,), (0,)), ((), ())), preferred_element_...  6.23 us
  transfers between devices with their start and end apart: 5, of which 4 were waited for; matrix products, arithmetic and copies ran while one was open for 15% of the time, Pallas kernels for 0%

commit v1 on v0

--- a/solution.py
+++ b/solution.py
@@ -57,7 +57,9 @@
     units = down_weight.shape[0]
     width = down_weight.shape[1]
     grad_replica = gathered_copies(grad_local, "col", 0)
-    grad_all = lax.all_gather(grad_replica[:, None, :], DP, axis=1, tiled=True)
+    grad_all = jnp.concatenate(
+        lax.all_to_all(jnp.stack([grad_replica[:, None, :]] * lax.axis_size(DP)), DP, 0, 0), axis=1
+    )
     tok_count = grad_all.shape[0]
     replica_count = grad_all.shape[1]
     local_tokens = hidden_local.shape[0]

time: 221 us -> 347 us (1.57)
  waiting for transfers between devices: 118 us -> 239 us
  starting transfers between devices: 19.8 us -> 40.1 us
  between operations: 14.1 us -> 0.75 us
  blocking collectives: 32.4 us -> 25.1 us
  local copies, waits for them, and re-layouts: 22.8 us -> 27.8 us
    all_to_all x0 -> x1, waiting for transfers between devices: none -> 188 us  [on_device(): lax.all_to_all(jnp.stack([grad_replica[:, None, :]] * lax.axis_size(DP)),...]
    all_gather x1 -> x0, waiting for transfers between devices: 65 us -> none  [on_device(): grad_all = lax.all_gather(grad_replica[:, None, :], DP, axis=1, tiled=True)]
    all_to_all x1, starting transfers between devices: 7.13 us -> 18.9 us  [on_device(): lax.all_to_all(local_grad, DP, split_axis=1, concat_axis=2, tiled=True)]
    all_gather x1 -> x0, local copies, waits for them, and re-layouts: 11.3 us -> none  [on_device(): grad_all = lax.all_gather(grad_replica[:, None, :], DP, axis=1, tiled=True)]
    all_to_all x0 -> x1, local copies, waits for them, and re-layouts: none -> 11.3 us  [on_device(): lax.all_to_all(jnp.stack([grad_replica[:, None, :]] * lax.axis_size(DP)),...]
    all_to_all x0 -> x1, starting transfers between devices: none -> 6.14 us  [on_device(): lax.all_to_all(jnp.stack([grad_replica[:, None, :]] * lax.axis_size(DP)),...]
    all_to_all x1 -> x0, blocking collectives: 4.65 us -> none  [sent_to_all(): lax.all_to_all(jnp.broadcast_to(value[None], (devices, *value.shape)), ax...]
    another operation x0 -> x1, local copies, waits for them, and re-layouts: none -> 4.29 us  [on_device(): jnp.stack([grad_replica[:, None, :]] * lax.axis_size(DP))]
  transfers between devices with their start and end apart: 5 -> 6, of which waited for: 4 -> 4; matrix products, arithmetic and copies ran while one was open for 15% -> 9% of each run, Pallas kernels for 0% -> 0%
where the time goes in v1:
time: 347 us; the launch traced here: 346 us
  waiting for transfers between devices  239 us (69%)
  starting transfers between devices  40.1 us (12%)
  local copies, waits for them, and re-layouts  27.8 us (8%)
  blocking collectives  25.1 us (7%)
  matrix products  12.3 us (4%)
    all_to_all x1, waiting for transfers between devices, on_device(): lax.all_to_all(jnp.stack([grad_replica[:, None, :]] * lax.axis_size(DP)),...  188 us
    all_to_all x1, blocking collectives, exchange_in_order(): out = lax.all_to_all(out, axes[k], k, k, tiled=True)  25.1 us
    all_to_all x1, waiting for transfers between devices, sent_and_summed(): lax.all_to_all(cut_along(value, dim, devices), axis, 0, 0, tiled=True)  21.5 us
    all_to_all x2, waiting for transfers between devices, sent_to_all(): lax.all_to_all(jnp.broadcast_to(value[None], (devices, *value.shape)), ax...  20.5 us
    all_to_all x1, starting transfers between devices, on_device(): lax.all_to_all(local_grad, DP, split_axis=1, concat_axis=2, tiled=True)  18.9 us
    all_to_all x1, local copies, waits for them, and re-layouts, on_device(): lax.all_to_all(jnp.stack([grad_replica[:, None, :]] * lax.axis_size(DP)),...  11.3 us
    all_to_all x1, waiting for transfers between devices, on_device(): lax.all_to_all(local_grad, DP, split_axis=1, concat_axis=2, tiled=True)  8.68 us
    all_to_all x2, starting transfers between devices, sent_to_all(): lax.all_to_all(jnp.broadcast_to(value[None], (devices, *value.shape)), ax...  7.23 us
  transfers between devices with their start and end apart: 6, of which 4 were waited for; matrix products, arithmetic and copies ran while one was open for 9% of the time, Pallas kernels for 0%

profile of v1, /device:TPU:32, one launch (start us, length us, event | category | flops | bytes accessed | tf_op | source)
XLA Modules:
  0.0 346.4 jit_solution(10180343884649840650)
XLA Ops:
  0.6 0.0 copy-start
  0.6 1.7 broadcast_in_dim.15
  2.3 3.4 all-to-all-start
  5.8 1.8 reshape_broadcast_in_dim_squeeze.3
  7.6 0.3 copy.27
  7.9 0.4 copy.28
  8.3 0.0 all-to-all-done
  8.3 25.1 %all_to_all.39 = bf16[8,4,32,1,224]{4,1,2,3,0:T(4,128)(2,1)S(1)} all-to-all(bf16[8,4,32,1,224]{4,1,2,3,0:T(4,128)(2,1)S(1)} %copy.28), channel_id=1, replica_groups=mesh['row'=4,'col'=2,'dp_0'=8,'dp_1'=4] {'dp_0'}, dimensions={0} | all-to-all | bytes 917504 | tf_op jit(solution)/shard_map/all_to_all | solution.py:39
  33.3 4.3 %stack.3 = bf16[32,128,1,1024]{3,1,2,0:T(8,128)(2,1)} broadcast(bf16[128,1024]{1,0:T(8,128)(2,1)S(1)} %bitcast.33), dimensions={1,3} | broadcast | bytes 8650752 | tf_op jit(solution)/shard_map/stack | solution.py:61
  37.6 6.1 %all-to-all-start.1 = ((bf16[32,128,1,1024]{3,1,2,0:T(8,128)(2,1)}), bf16[32,128,1,1024]{3,1,2,0:T(8,128)(2,1)}, u32[]{:S(2)}, u32[]{:S(2)}) async-start(bf16[32,128,1,1024]{3,1,2,0:T(8,128)(2,1)} %stack.3), calls=%async_computation.1 | async-start | bytes 16777216 | tf_op jit(solution)/shard_map/all_to_all | solution.py:61
  43.8 1.1 copy.29
  44.9 187.9 %all-to-all-done.1 = bf16[32,128,1,1024]{3,1,2,0:T(8,128)(2,1)} async-done(((bf16[32,128,1,1024]{3,1,2,0:T(8,128)(2,1)}), bf16[32,128,1,1024]{3,1,2,0:T(8,128)(2,1)}, u32[]{:S(2)}, u32[]{:S(2)}) %all-to-all-start.1) | async-done | bytes 8388640 | tf_op jit(solution)/shard_map/all_to_all | solution.py:61
  232.8 3.5 %all-to-all-start.5 = ((bf16[8,4,32,1,224]{4,0,2,3,1:T(8,128)(2,1)}), bf16[8,4,32,1,224]{4,0,2,3,1:T(8,128)(2,1)S(1)}, u32[]{:S(2)}, u32[]{:S(2)}) async-start(bf16[8,4,32,1,224]{4,0,2,3,1:T(8,128)(2,1)} %copy.29), calls=%async_computation.5 | async-start | bytes 1048576 | tf_op jit(solution)/shard_map/all_to_all | solution.py:39
  236.3 11.3 %copy.21 = bf16[32,128,1,1024]{3,0,1,2:T(8,128)(2,1)} copy(bf16[32,128,1,1024]{3,1,2,0:T(8,128)(2,1)} %all-to-all-done.1) | data formatting | bytes 16777216 | tf_op jit(solution)/shard_map/all_to_all | solution.py:61
  247.6 0.0 copy-done
  247.6 6.0 %convolution_convert_fusion = bf16[4096,224]{0,1:T(8,128)(2,1)S(1)} fusion(bf16[4096,1024]{1,0:T(8,128)(2,1)} %bitcast.23, bf16[224,1024]{1,0:T(8,128)(2,1)S(1)} %copy-done), kind=kOutput, calls=%fused_computation | convolution fusion | flops 1879965696 | bytes 10682368 | tf_op jit(solution)/shard_map/dot_general | solution.py:71
  253.6 1.5 copy.36
  255.1 0.0 all-to-all-done.5
  255.1 4.3 %all-to-all-start.2 = ((bf16[4,1024,224]{1,2,0:T(8,128)(2,1)}), bf16[4,1024,224]{1,2,0:T(8,128)(2,1)S(1)}, u32[]{:S(2)}, u32[]{:S(2)}) async-start(bf16[4,1024,224]{1,2,0:T(8,128)(2,1)} %bitcast.26), calls=%async_computation.2 | async-start | bytes 3670016 | tf_op jit(solution)/shard_map/all_to_all | solution.py:50
  259.4 0.1 copy.30
  259.5 0.3 copy.37
  259.8 21.5 %all-to-all-done.2 = bf16[4,1024,224]{1,2,0:T(8,128)(2,1)S(1)} async-done(((bf16[4,1024,224]{1,2,0:T(8,128)(2,1)}), bf16[4,1024,224]{1,2,0:T(8,128)(2,1)S(1)}, u32[]{:S(2)}, u32[]{:S(2)}) %all-to-all-start.2) | async-done | bytes 1835040 | tf_op jit(solution)/shard_map/all_to_all | solution.py:50
  281.3 0.0 copy-start.1
  281.3 1.8 broadcast_in_dim.17
  283.1 0.1 copy-done.1
  283.2 3.8 %all-to-all-start.6 = ((bf16[4,32,32,224]{3,2,1,0:T(8,128)(2,1)}), bf16[4,32,32,224]{3,2,1,0:T(8,128)(2,1)S(1)}, u32[]{:S(2)}, u32[]{:S(2)}) async-start(bf16[4,32,32,224]{3,2,1,0:T(8,128)(2,1)} %broadcast_in_dim.17), calls=%async_computation.6 | async-start | bytes 4194304 | tf_op jit(solution)/shard_map/all_to_all | solution.py:13
  287.0 1.9 reduce_sum.12
  288.8 0.2 copy.24
  289.0 1.1 copy.25
  290.1 20.5 %all-to-all-done.6 = bf16[4,32,32,224]{3,2,1,0:T(8,128)(2,1)S(1)} async-done(((bf16[4,32,32,224]{3,2,1,0:T(8,128)(2,1)}), bf16[4,32,32,224]{3,2,1,0:T(8,128)(2,1)S(1)}, u32[]{:S(2)}, u32[]{:S(2)}) %all-to-all-start.6) | async-done | bytes 1835040 | tf_op jit(solution)/shard_map/all_to_all | solution.py:13
  310.6 18.9 %all-to-all-start.3 = ((bf16[32,32,224]{2,0,1:T(8,128)(2,1)}), bf16[32,32,224]{2,0,1:T(8,128)(2,1)S(1)}, u32[]{:S(2)}, u32[]{:S(2)}) async-start(bf16[32,32,224]{2,0,1:T(8,128)(2,1)} %copy.25), calls=%async_computation.3 | async-start | bytes 1048576 | tf_op jit(solution)/shard_map/all_to_all | solution.py:78
  329.5 6.2 %fusion = bf16[224,1024]{1,0:T(8,128)(2,1)} fusion(bf16[4096,224]{1,0:T(8,128)(2,1)S(1)} %bitcast.25, bf16[4096,1024]{1,0:T(8,128)(2,1)} %bitcast.24), kind=kOutput, calls=%fused_computation.3 | convolution fusion | flops 1879506944 | bytes 10682368 | tf_op jit(solution)/shard_map/dot_general | solution.py:83
  335.8 8.7 %all-to-all-done.3 = bf16[32,32,224]{2,0,1:T(8,128)(2,1)S(1)} async-done(((bf16[32,32,224]{2,0,1:T(8,128)(2,1)}), bf16[32,32,224]{2,0,1:T(8,128)(2,1)S(1)}, u32[]{:S(2)}, u32[]{:S(2)}) %all-to-all-start.3) | async-done | bytes 458784 | tf_op jit(solution)/shard_map/all_to_all | solution.py:78
  344.4 0.3 copy.26
  344.7 1.6 reshape.34
Async XLA Ops:
  0.6 246.9 %copy-start = (bf16[224,1024]{1,0:T(8,128)(2,1)S(1)}, bf16[224,1024]{1,0:T(8,128)(2,1)}, u32[]{:S(2)}) copy-start(bf16[224,1024]{1,0:T(8,128)(2,1)} %param.5) | copy-start | bytes 1376260
  2.3 5.9 %all-to-all-start = ((bf16[2,64,1024]{2,1,0:T(8,128)(2,1)}), bf16[2,64,1024]{2,1,0:T(8,128)(2,1)S(1)}, u32[]{:S(2)}, u32[]{:S(2)}) async-start(bf16[2,64,1024]{2,1,0:T(8,128)(2,1)} %broadcast_in_dim.15), calls=%async_computation | async-start | bytes 524288 | tf_op jit(solution)/shard_map/all_to_all | solution.py:13
  37.6 195.1 %all-to-all-start.1 = ((bf16[32,128,1,1024]{3,1,2,0:T(8,128)(2,1)}), bf16[32,128,1,1024]{3,1,2,0:T(8,128)(2,1)}, u32[]{:S(2)}, u32[]{:S(2)}) async-start(bf16[32,128,1,1024]{3,1,2,0:T(8,128)(2,1)} %stack.3), calls=%async_computation.1 | async-start | bytes 16777216 | tf_op jit(solution)/shard_map/all_to_all | solution.py:61
  232.8 22.3 %all-to-all-start.5 = ((bf16[8,4,32,1,224]{4,0,2,3,1:T(8,128)(2,1)}), bf16[8,4,32,1,224]{4,0,2,3,1:T(8,128)(2,1)S(1)}, u32[]{:S(2)}, u32[]{:S(2)}) async-start(bf16[8,4,32,1,224]{4,0,2,3,1:T(8,128)(2,1)} %copy.29), calls=%async_computation.5 | async-start | bytes 1048576 | tf_op jit(solution)/shard_map/all_to_all | solution.py:39
  255.1 26.2 %all-to-all-start.2 = ((bf16[4,1024,224]{1,2,0:T(8,128)(2,1)}), bf16[4,1024,224]{1,2,0:T(8,128)(2,1)S(1)}, u32[]{:S(2)}, u32[]{:S(2)}) async-start(bf16[4,1024,224]{1,2,0:T(8,128)(2,1)} %bitcast.26), calls=%async_computation.2 | async-start | bytes 3670016 | tf_op jit(solution)/shard_map/all_to_all | solution.py:50
  281.3 1.9 copy-start.1
  283.2 27.4 %all-to-all-start.6 = ((bf16[4,32,32,224]{3,2,1,0:T(8,128)(2,1)}), bf16[4,32,32,224]{3,2,1,0:T(8,128)(2,1)S(1)}, u32[]{:S(2)}, u32[]{:S(2)}) async-start(bf16[4,32,32,224]{3,2,1,0:T(8,128)(2,1)} %broadcast_in_dim.17), calls=%async_computation.6 | async-start | bytes 4194304 | tf_op jit(solution)/shard_map/all_to_all | solution.py:13
  310.6 33.8 %all-to-all-start.3 = ((bf16[32,32,224]{2,0,1:T(8,128)(2,1)}), bf16[32,32,224]{2,0,1:T(8,128)(2,1)S(1)}, u32[]{:S(2)}, u32[]{:S(2)}) async-start(bf16[32,32,224]{2,0,1:T(8,128)(2,1)} %copy.25), calls=%async_computation.3 | async-start | bytes 1048576 | tf_op jit(solution)/shard_map/all_to_all | solution.py:78
